TPU v7x, 32 devices: a whole 2x2x4 slice. The times are simulated.
32 devices in a mesh: owner: 4 (over y, x), rows: 8 (over z, core).
Axes of the slice: x: 2, y: 2, z: 4, core: 2. Of those that a mesh axis runs over, the one named last changes fastest.
Arguments:
- w_gate: float32 [64, 2048, 1024], P('owner', 'rows'), may hold values from -0.1875 to 0.1875
- avg_gate: bfloat16 [64, 2048, 1024], P('owner', 'rows'), may hold values from -0.0625 to 0.0625
- w_up: float32 [64, 2048, 1024], P('owner', 'rows'), may hold values from -0.1875 to 0.1875
- avg_up: bfloat16 [64, 2048, 1024], P('owner', 'rows'), may hold values from -0.0625 to 0.0625
- w_down: float32 [64, 1024, 2048], P('owner', None, 'rows'), may hold values from -0.25 to 0.25
- avg_down: bfloat16 [64, 1024, 2048], P('owner', None, 'rows'), may hold values from -0.09375 to 0.09375
- router_weight: float32 [2048, 64], P('rows', 'owner'), may hold values from -0.125 to 0.125
- router_gain: float32 [2048], P('rows'), may hold values from 0.25 to 1.75
Outputs:
- serve_gate: bfloat16 [64, 2048, 1024], P('owner', None, 'rows')
- serve_up: bfloat16 [64, 2048, 1024], P('owner', None, 'rows')
- serve_down: bfloat16 [64, 1024, 2048], P('owner', 'rows')
- scale_gate: float32 [64, 1024], P('owner', 'rows')
- scale_up: float32 [64, 1024], P('owner', 'rows')
- scale_down: float32 [64, 1024], P('owner', 'rows')
- serve_router: bfloat16 [2048, 64], replicated
All inputs are finite; a program needn't handle non-finite values.
Results may differ from a plain program's by a relative error of at most 0.0015.
Values may be sent and summed in bfloat16 or wider, within the bound.
A program may use at most 192 MiB of HBM per device.

v0:
```python
import jax
import jax.numpy as jnp
from jax import lax
from jax.sharding import PartitionSpec as P


def shards(w_gate, avg_gate, w_up, avg_up, w_down, avg_down, router_weight, router_gain):
    fresh_gate = w_gate + avg_gate.astype(jnp.float32)
    fresh_up = w_up + avg_up.astype(jnp.float32)
    fresh_down = w_down + avg_down.astype(jnp.float32)
    total_gate, total_up, total_down = lax.psum(
        (
            jnp.sum(fresh_gate * fresh_gate, axis=1),
            jnp.sum(fresh_up * fresh_up, axis=1),
            jnp.sum(fresh_down * fresh_down, axis=2),
        ),
        "rows",
    )
    scale_gate = jnp.sqrt(total_gate)
    scale_up = jnp.sqrt(total_up)
    scale_down = jnp.sqrt(total_down)
    narrow_gate, narrow_up, narrow_down = (
        (fresh_gate / jnp.expand_dims(scale_gate, 1)).astype(jnp.bfloat16),
        (fresh_up / jnp.expand_dims(scale_up, 1)).astype(jnp.bfloat16),
        (fresh_down / jnp.expand_dims(scale_down, 2)).astype(jnp.bfloat16),
    )
    serve_gate, serve_up = (
        lax.all_to_all(narrow_gate, "rows", split_axis=2, concat_axis=1, tiled=True),
        lax.all_to_all(narrow_up, "rows", split_axis=2, concat_axis=1, tiled=True),
    )
    serve_down = lax.all_to_all(narrow_down, "rows", split_axis=1, concat_axis=2, tiled=True)
    scale_gate = lax.dynamic_slice_in_dim(
        scale_gate, lax.axis_index("rows") * serve_gate.shape[2], serve_gate.shape[2], axis=1
    )
    scale_up = lax.dynamic_slice_in_dim(
        scale_up, lax.axis_index("rows") * serve_up.shape[2], serve_up.shape[2], axis=1
    )
    scale_down = lax.dynamic_slice_in_dim(
        scale_down, lax.axis_index("rows") * serve_down.shape[1], serve_down.shape[1], axis=1
    )
    part_router = (router_weight * router_gain[:, None]).astype(jnp.bfloat16)
    row_router = lax.all_gather(part_router, "rows", axis=0, tiled=True)
    serve_router = lax.all_gather(row_router, "owner", axis=1, tiled=True)
    return (serve_gate, serve_up, serve_down, scale_gate, scale_up, scale_down, serve_router)


def solution(mesh):
    return jax.shard_map(
        shards,
        mesh=mesh,
        in_specs=(
            P("owner", "rows", None),
            P("owner", "rows", None),
            P("owner", "rows", None),
            P("owner", "rows", None),
            P("owner", None, "rows"),
            P("owner", None, "rows"),
            P("rows", "owner"),
            P("rows"),
        ),
        out_specs=(
            P("owner", None, "rows"),
            P("owner", None, "rows"),
            P("owner", "rows", None),
            P("owner", "rows"),
            P("owner", "rows"),
            P("owner", "rows"),
            P(),
        ),
        check_vma=False,
    )
```

profile of v0, /device:TPU:0, one launch (start us, length us, event | category | flops | bytes accessed | tf_op | source)
XLA Modules:
  0.0 824.8 jit_solution(4685212397091970850)
XLA Ops:
  7.2 0.0 all-reduce.3.cloned.1.call-start
  7.2 17.6 %copy.31 = f32[16,256,1024]{1,0,2:T(8,128)} copy(f32[16,256,1024]{2,1,0:T(8,128)} %param.8) | data formatting | bytes 33554432 | tf_op args[0]
  24.8 17.6 %copy.34 = f32[16,256,1024]{1,0,2:T(8,128)} copy(f32[16,256,1024]{2,1,0:T(8,128)} %param.10) | data formatting | bytes 33554432 | tf_op args[2]
  42.4 12.5 %copy.30 = bf16[16,256,1024]{1,0,2:T(8,128)(2,1)} copy(bf16[16,256,1024]{2,1,0:T(8,128)(2,1)} %param.9) | data formatting | bytes 16777216 | tf_op args[1]
  54.9 12.5 %copy.33 = bf16[16,256,1024]{1,0,2:T(8,128)(2,1)} copy(bf16[16,256,1024]{2,1,0:T(8,128)(2,1)} %param.11) | data formatting | bytes 16777216 | tf_op args[3]
  67.4 0.0 copy-start
  67.4 0.0 copy-start.1
  67.4 25.2 %multiply_reduce_fusion = f32[16,1024]{0,1:T(8,128)} fusion(f32[16,1024,256]{2,1,0:T(8,128)} %param.12, bf16[16,1024,256]{2,1,0:T(8,128)(2,1)} %param.13), kind=kLoop, calls=%fused_computation.2 | loop fusion | flops 16760832 | bytes 25231360 | tf_op jit(solution)/shard_map/reduce_sum | solution.py:15
  92.6 0.0 copy-done
  92.6 0.0 copy-done.1
  92.6 13.2 %multiply_reduce_fusion.1 = (f32[16,1024]{0,1:T(8,128)}, f32[16,1024]{0,1:T(8,128)}) fusion(f32[16,256,1024]{1,0,2:T(8,128)} %copy.34, bf16[16,256,1024]{1,0,2:T(8,128)(2,1)S(1)} %copy-done.1, f32[16,256,1024]{1,0,2:T(8,128)} %copy.31, bf16[16,256,1024]{1,0,2:T(8,128)(2,1)S(1)} %copy-done), kind=kLoop, calls=%fused_computation.4 | loop fusion | flops 33521664 | bytes 50462720 | tf_op jit(solution)/shard_map/reduce_sum | solution.py:14
  105.8 0.0 all-reduce.3.cloned.1.call-update
  105.8 65.1 %all-reduce.3.cloned.1.call-done = (f32[16,1024]{0,1:T(8,128)}, f32[16,1024]{0,1:T(8,128)}, f32[16,1024]{0,1:T(8,128)}) async-done(((f32[16,1024]{0,1:T(8,128)}, f32[16,1024]{0,1:T(8,128)}, f32[16,1024]{0,1:T(8,128)}), (f32[16,1024]{0,1:T(8,128)}, f32[16,1024]{0,1:T(8,128)}, f32[16,1024]{0,1:T(8,128)})) %all-reduce.3.cloned.1.call-update) | async-done | bytes 196624 | tf_op jit(solution)/shard_map/psum | solution.py:11
  170.9 1.2 sqrt.10
  172.1 12.0 %divide_convert_fusion.1 = bf16[16,256,1024]{1,0,2:T(8,128)(2,1)} fusion(f32[16,256,1024]{1,0,2:T(8,128)} %copy.34, bf16[16,256,1024]{1,0,2:T(8,128)(2,1)} %copy.33, f32[16,1024]{0,1:T(8,128)S(1)} %sqrt.10), kind=kLoop, calls=%fused_computation.3 | loop fusion | flops 16777216 | bytes 33619968 | tf_op jit(solution)/shard_map/convert_element_type | solution.py:24
  184.1 0.0 copy-start.3
  184.1 5.1 all-to-all-start.1
  189.2 0.0 copy-done.3
  189.2 0.1 sqrt.9
  189.3 12.0 %divide_convert_fusion.2 = bf16[16,256,1024]{1,0,2:T(8,128)(2,1)} fusion(f32[16,256,1024]{1,0,2:T(8,128)} %copy.31, bf16[16,256,1024]{1,0,2:T(8,128)(2,1)} %copy.30, f32[16,1024]{0,1:T(8,128)S(1)} %sqrt.9), kind=kLoop, calls=%fused_computation.6 | loop fusion | flops 16777216 | bytes 33619968 | tf_op jit(solution)/shard_map/convert_element_type | solution.py:23
  201.3 0.0 copy-start.2
  201.3 171.7 %all-to-all-done.1 = bf16[16,256,1024]{1,0,2:T(8,128)(2,1)} async-done(((bf16[16,256,1024]{1,0,2:T(8,128)(2,1)}), bf16[16,256,1024]{1,0,2:T(8,128)(2,1)}, u32[]{:S(2)}, u32[]{:S(2)}) %all-to-all-start.1) | async-done | bytes 8388640 | tf_op jit(solution)/shard_map/all_to_all | solution.py:29
  373.0 5.1 all-to-all-start
  378.2 0.0 copy-done.2
  378.2 0.1 sqrt.11
  378.3 23.8 %divide_convert_fusion = bf16[16,1024,256]{2,0,1:T(8,128)(2,1)} fusion(f32[16,1024,256]{2,1,0:T(8,128)} %param.12, f32[16,1024]{0,1:T(8,128)S(1)} %sqrt.11, bf16[16,1024,256]{2,1,0:T(8,128)(2,1)} %param.13), kind=kLoop, calls=%fused_computation.1 | loop fusion | flops 16777216 | bytes 33619968 | tf_op jit(solution)/shard_map/convert_element_type | solution.py:25
  402.1 0.0 copy-start.4
  402.1 0.0 copy-start.5
  402.1 159.8 %all-to-all-done = bf16[16,256,1024]{1,0,2:T(8,128)(2,1)} async-done(((bf16[16,256,1024]{1,0,2:T(8,128)(2,1)}), bf16[16,256,1024]{1,0,2:T(8,128)(2,1)}, u32[]{:S(2)}, u32[]{:S(2)}) %all-to-all-start) | async-done | bytes 8388640 | tf_op jit(solution)/shard_map/all_to_all | solution.py:28
  561.8 5.0 all-to-all-start.2
  566.9 0.0 copy-done.4
  566.9 0.0 copy-done.5
  566.9 189.9 %all_gather.6 = bf16[2048,16]{0,1:T(8,128)(2,1)S(1)} all-gather(bf16[256,16]{0,1:T(8,128)(2,1)S(1)} %multiply_convert_fusion), channel_id=1, replica_groups=mesh['owner'=4,'rows'=8] {'rows'}, dimensions={0}, use_global_device_ids=true | all-gather | bytes 73728 | tf_op jit(solution)/shard_map/all_gather | solution.py:42
  756.8 9.1 %all_gather.7 = bf16[2048,64]{0,1:T(8,128)(2,1)S(1)} all-gather(bf16[2048,16]{0,1:T(8,128)(2,1)S(1)} %all_gather.6), channel_id=1, replica_groups=mesh['owner'=4,'rows'=8] {'owner'}, dimensions={1}, use_global_device_ids=true | all-gather | bytes 327680 | tf_op jit(solution)/shard_map/all_gather | solution.py:43
  765.9 0.7 copy.39
  766.6 0.7 copy.40
  767.3 0.7 copy.41
  767.9 12.3 %copy.35 = bf16[16,8,256,128]{3,2,1,0:T(8,128)(2,1)} copy(bf16[16,8,256,128]{2,0,3,1:T(8,128)(2,1)} %bitcast.4) | data formatting | bytes 16777216 | tf_op jit(solution)/shard_map/all_to_all | solution.py:29
  780.2 12.3 %copy.32 = bf16[16,8,256,128]{3,2,1,0:T(8,128)(2,1)} copy(bf16[16,8,256,128]{2,0,3,1:T(8,128)(2,1)} %bitcast.1) | data formatting | bytes 16777216 | tf_op jit(solution)/shard_map/all_to_all | solution.py:28
  792.5 0.0 all-to-all-done.2
  792.5 11.4 %copy.38 = bf16[16,128,8,256]{3,2,1,0:T(8,128)(2,1)} copy(bf16[16,128,8,256]{3,0,1,2:T(8,128)(2,1)} %bitcast.7) | data formatting | bytes 16777216 | tf_op jit(solution)/shard_map/all_to_all | solution.py:31
  803.9 13.4 %all_to_all.50 = bf16[16,128,2048]{2,1,0:T(8,128)(2,1)} reshape(bf16[16,128,8,256]{3,2,1,0:T(8,128)(2,1)} %copy.38) | data formatting | bytes 16777216 | tf_op jit(solution)/shard_map/all_to_all | solution.py:31
  817.3 0.7 copy.53
  (4 shorter events, 0.0 us)
Async XLA Ops:
  7.2 163.7 %all-reduce.3.cloned.1.call-start = ((), (), s32[]{:S(2)}) async-start(), calls=%async_computation.3 | async-start | bytes 3145728 | tf_op jit(solution)/shard_map/psum | solution.py:11
  67.4 25.2 %copy-start = (bf16[16,256,1024]{1,0,2:T(8,128)(2,1)S(1)}, bf16[16,256,1024]{1,0,2:T(8,128)(2,1)}, u32[]{:S(2)}) copy-start(bf16[16,256,1024]{1,0,2:T(8,128)(2,1)} %copy.30) | copy-start | bytes 25165828
  67.4 25.2 %copy-start.1 = (bf16[16,256,1024]{1,0,2:T(8,128)(2,1)S(1)}, bf16[16,256,1024]{1,0,2:T(8,128)(2,1)}, u32[]{:S(2)}) copy-start(bf16[16,256,1024]{1,0,2:T(8,128)(2,1)} %copy.33) | copy-start | bytes 25165828
  184.1 5.1 copy-start.3
  184.1 189.0 %all-to-all-start.1 = ((bf16[16,256,1024]{1,0,2:T(8,128)(2,1)}), bf16[16,256,1024]{1,0,2:T(8,128)(2,1)}, u32[]{:S(2)}, u32[]{:S(2)}) async-start(bf16[16,256,1024]{1,0,2:T(8,128)(2,1)} %divide_convert_fusion.1), calls=%async_computation.1 | async-start | bytes 16777216 | tf_op jit(solution)/shard_map/all_to_all | solution.py:29
  201.3 176.9 %copy-start.2 = (f32[16,1024]{0,1:T(8,128)S(1)}, f32[16,1024]{0,1:T(8,128)}, u32[]{:S(2)}) copy-start(f32[16,1024]{0,1:T(8,128)} %get-tuple-element.16) | copy-start | bytes 196612
  373.0 188.8 %all-to-all-start = ((bf16[16,256,1024]{1,0,2:T(8,128)(2,1)}), bf16[16,256,1024]{1,0,2:T(8,128)(2,1)}, u32[]{:S(2)}, u32[]{:S(2)}) async-start(bf16[16,256,1024]{1,0,2:T(8,128)(2,1)} %divide_convert_fusion.2), calls=%async_computation | async-start | bytes 16777216 | tf_op jit(solution)/shard_map/all_to_all | solution.py:28
  402.1 164.8 %copy-start.4 = (f32[256,16]{0,1:T(8,128)S(1)}, f32[256,16]{0,1:T(8,128)}, u32[]{:S(2)}) copy-start(f32[256,16]{0,1:T(8,128)} %param.14) | copy-start | bytes 49156
  402.1 164.8 %copy-start.5 = (f32[256]{0:T(256)S(1)}, f32[256]{0:T(256)}, u32[]{:S(2)}) copy-start(f32[256]{0:T(256)} %param.15) | copy-start | bytes 3076
  561.8 230.7 %all-to-all-start.2 = ((bf16[16,1024,256]{2,0,1:T(8,128)(2,1)}), bf16[16,1024,256]{2,0,1:T(8,128)(2,1)}, u32[]{:S(2)}, u32[]{:S(2)}) async-start(bf16[16,1024,256]{2,0,1:T(8,128)(2,1)} %divide_convert_fusion), calls=%async_computation.2 | async-start | bytes 16777216 | tf_op jit(solution)/shard_map/all_to_all | solution.py:31
Sparse Core Ops, SparseCore 0:
  105.9 64.9 all-reduce.2
where the time goes:
time: 827 us; the launch traced here: 825 us
  waiting for transfers between devices  397 us (48%)
  blocking collectives  199 us (24%)
  local copies, waits for them, and re-layouts  114 us (14%)
  other arithmetic  86.1 us (10%)
  starting transfers between devices  15.3 us (2%)
  between operations  14.1 us (2%)
    all_gather x1, blocking collectives, shards(): row_router = lax.all_gather(part_router, 'rows', axis=0, tiled=True)  190 us
    all_to_all x1, waiting for transfers between devices, shards(): lax.all_to_all(narrow_up, 'rows', split_axis=2, concat_axis=1, tiled=True)  172 us
    all_to_all x1, waiting for transfers between devices, shards(): lax.all_to_all(narrow_gate, 'rows', split_axis=2, concat_axis=1, tiled=True)  160 us
    psum x1, waiting for transfers between devices, shards(): lax.psum((jnp.sum(fresh_gate * fresh_gate, axis=1), jnp.sum(fresh_up * fr...  65.1 us
    unnamed x20, local copies, waits for them, and re-layouts  62.9 us
    reduce_sum x1, other arithmetic, shards(): jnp.sum(fresh_down * fresh_down, axis=2)  25.2 us
    all_to_all x2, local copies, waits for them, and re-layouts, shards(): lax.all_to_all(narrow_down, 'rows', split_axis=1, concat_axis=2, tiled=True)  24.8 us
    convert_element_type x1, other arithmetic, shards(): (fresh_down / jnp.expand_dims(scale_down, 2)).astype(jnp.bfloat16)  23.8 us
  transfers between devices with their start and end apart: 4, of which 3 were waited for; matrix products, arithmetic and copies ran while one was open for 8% of the time, Pallas kernels for 0%

commit v1 on v0

v1 whole, which is shorter than its diff:
```python
import jax
import jax.numpy as jnp
from jax import lax
from jax.experimental import pallas as pl
from jax.experimental.pallas import tpu as pltpu
from jax.sharding import PartitionSpec as P

LANES = 128
STEP = 4


def columns_sum(w, a, o):
    @pl.loop(0, w.shape[0])
    def _(e):
        fresh = w[e] + a[e].astype(jnp.float32)
        o[e] = jnp.sum(fresh * fresh, axis=0, keepdims=True)


def rows_sum(w, a, o):
    @pl.loop(0, w.shape[0])
    def _(e):
        fresh = w[e] + a[e].astype(jnp.float32)
        square = fresh * fresh
        folded = square[:, :LANES]
        for start in range(LANES, square.shape[1], LANES):
            folded = folded + square[:, start : start + LANES]
        o[e] = jnp.sum(folded.T, axis=0, keepdims=True)


def columns_norm(w, a, s, *refs):
    o = refs[-1]

    @pl.loop(0, w.shape[0])
    def _(e):
        fresh = (w[e] + a[e].astype(jnp.float32)) * (1.0 / s[e])
        for part in range(o.shape[0]):
            o[part, e] = fresh[:, part * LANES : (part + 1) * LANES].astype(o.dtype)


def rows_norm(w, a, s, *refs):
    o = refs[-1]
    height = w.shape[1] // o.shape[0]

    @pl.loop(0, w.shape[0])
    def _(e):
        inverse = 1.0 / s[e]
        for part in range(o.shape[0]):
            rows = slice(part * height, (part + 1) * height)
            factor = jnp.broadcast_to(inverse[:, rows], (LANES, height)).T
            for piece in range(w.shape[2] // LANES):
                lanes = slice(piece * LANES, (piece + 1) * LANES)
                fresh = w[e, rows, lanes] + a[e, rows, lanes].astype(jnp.float32)
                o[part, e, piece * height : (piece + 1) * height, :] = (fresh * factor).astype(o.dtype)


def stack_rows(x, *refs):
    o = refs[-1]
    height = x.shape[2]

    @pl.loop(0, x.shape[1])
    def _(e):
        for part in range(x.shape[0]):
            o[e, part * height : (part + 1) * height, :] = x[part, e]


def stack_columns(x, *refs):
    o = refs[-1]
    height = o.shape[1]
    pieces = x.shape[2] // height

    @pl.loop(0, x.shape[1])
    def _(e):
        for part in range(x.shape[0]):
            for piece in range(pieces):
                start = (part * pieces + piece) * LANES
                o[e, :, start : start + LANES] = x[part, e, piece * height : (piece + 1) * height, :]


def per_expert(shape, first=0):
    return pl.BlockSpec((STEP,) + shape[1:], lambda e: (e + first // STEP, 0, 0))


def per_expert_parts(shape, first=0):
    return pl.BlockSpec((shape[0], STEP) + shape[2:], lambda e: (0, e + first // STEP, 0, 0))


def call(body, count, inputs, specs, out, out_spec, held):
    aliases = {}
    if held is not None:
        aliases = {len(inputs): 0}
        inputs, specs = (*inputs, held), (*specs, pl.BlockSpec(memory_space=pl.ANY))
    moved = int(count * 2**21)
    return pl.pallas_call(
        body,
        grid=(count // STEP,),
        in_specs=list(specs),
        out_specs=out_spec,
        out_shape=out,
        input_output_aliases=aliases,
        cost_estimate=pl.CostEstimate(flops=moved, bytes_accessed=moved, transcendentals=0),
        compiler_params=pltpu.CompilerParams(
            dimension_semantics=("arbitrary",), vmem_limit_bytes=50 * 2**20
        ),
    )(*inputs)


def partial_sums(body, w, a, length, first, count):
    out = jax.ShapeDtypeStruct((count, 1, length), jnp.float32)
    specs = (per_expert(w.shape, first), per_expert(a.shape, first))
    return call(body, count, (w, a), specs, out, per_expert(out.shape), None)


def normalised(body, w, a, first, scale, scale_first, count, shape, slot=0, held=None):
    out = jax.ShapeDtypeStruct(shape, jnp.bfloat16)
    specs = (per_expert(w.shape, first), per_expert(a.shape, first), per_expert(scale.shape, scale_first))
    return call(body, count, (w, a, scale), specs, out, per_expert_parts(shape, slot), held)


def placed(body, x, slot, count, shape, first=0, held=None):
    out = jax.ShapeDtypeStruct(shape, jnp.bfloat16)
    return call(body, count, (x,), (per_expert_parts(x.shape, slot),), out, per_expert(shape, first), held)


def exchanged(x):
    return lax.all_to_all(x, "rows", split_axis=0, concat_axis=0, tiled=True)


def shards(parts, w_gate, avg_gate, w_up, avg_up, w_down, avg_down, router_weight, router_gain):
    experts, high, wide = w_gate.shape
    tall, deep = w_down.shape[1:]
    block, slab = wide // parts, tall // parts
    rank = lax.axis_index("rows")
    early = experts * 3 // 4 // STEP * STEP
    late = experts // 2 // STEP * STEP
    kept = experts - early

    part_router = (router_weight * router_gain[:, None]).astype(jnp.bfloat16).astype(jnp.float32).T
    columns, rows = part_router.shape
    head = partial_sums(columns_sum, w_gate, avg_gate, wide, 0, early)
    gathered = lax.all_gather(
        jnp.concatenate((head, part_router.reshape(-1, 1, wide))), "rows"
    )
    scale_head = jnp.sqrt(jnp.sum(gathered[:, :early], axis=0))
    row_router = gathered[:, early:].reshape(parts, columns, rows)

    send_a = normalised(
        columns_norm, w_gate, avg_gate, 0, scale_head, 0, early, (parts, early, high, block)
    )
    send_a, w_up, avg_up, w_down, avg_down, w_gate, avg_gate = lax.optimization_barrier(
        (send_a, w_up, avg_up, w_down, avg_down, w_gate, avg_gate)
    )
    got_a = exchanged(send_a)

    part_rest = partial_sums(columns_sum, w_gate, avg_gate, wide, early, kept)
    part_up = partial_sums(columns_sum, w_up, avg_up, wide, 0, experts)
    part_down = partial_sums(rows_sum, w_down, avg_down, tall, 0, experts)
    total_columns, total_down = lax.psum(
        (jnp.concatenate((part_up, part_rest)), part_down), "rows"
    )
    scale_columns, scale_down = jnp.sqrt(total_columns), jnp.sqrt(total_down)
    scale_up, scale_rest = scale_columns[:experts], scale_columns[experts:]
    shape_b = (parts, kept + experts + late, high, block)
    send_b = normalised(columns_norm, w_gate, avg_gate, early, scale_columns, experts, kept, shape_b)
    send_b = normalised(columns_norm, w_up, avg_up, 0, scale_columns, 0, experts, shape_b, kept, send_b)
    send_b = normalised(
        rows_norm, w_down, avg_down, 0, scale_down, 0, late, shape_b, kept + experts, send_b
    )
    send_b, scale_last = lax.optimization_barrier((send_b, scale_down))
    got_b = exchanged(send_b)

    last = experts - late
    send_c = normalised(
        rows_norm, w_down, avg_down, late, scale_last, late, last, (parts, last, high, block)
    )
    shape_columns = (experts, high * parts, block)
    shape_down = (experts, slab, deep * parts)
    serve_gate = placed(stack_rows, got_a, 0, early, shape_columns)
    row_router, send_c = lax.optimization_barrier((row_router, send_c))
    got_c = exchanged(send_c)
    row_router = row_router.transpose(1, 0, 2).reshape(columns, parts * rows).astype(jnp.bfloat16)
    serve_router = lax.all_gather(row_router, "owner", axis=0, tiled=True).T

    serve_gate = placed(stack_rows, got_b, 0, kept, shape_columns, early, serve_gate)
    serve_up = placed(stack_rows, got_b, kept, experts, shape_columns)
    serve_down = placed(stack_columns, got_b, kept + experts, late, shape_down)
    serve_down = placed(stack_columns, got_c, 0, last, shape_down, late, serve_down)

    def own(scale, width):
        return lax.dynamic_slice_in_dim(scale[:, 0, :], rank * width, width, axis=1)

    return (
        serve_gate,
        serve_up,
        serve_down,
        own(jnp.concatenate((scale_head, scale_rest)), block),
        own(scale_up, block),
        own(scale_down, slab),
        serve_router,
    )


def plain_shards(w_gate, avg_gate, w_up, avg_up, w_down, avg_down, router_weight, router_gain):
    def served(w, a, axis, split):
        fresh = w + a.astype(jnp.float32)
        scale = jnp.sqrt(lax.psum(jnp.sum(fresh * fresh, axis=axis), "rows"))
        narrow = (fresh / jnp.expand_dims(scale, axis)).astype(jnp.bfloat16)
        serve = lax.all_to_all(narrow, "rows", split_axis=split, concat_axis=axis, tiled=True)
        width = serve.shape[split]
        return serve, lax.dynamic_slice_in_dim(scale, lax.axis_index("rows") * width, width, axis=1)

    serve_gate, scale_gate = served(w_gate, avg_gate, 1, 2)
    serve_up, scale_up = served(w_up, avg_up, 1, 2)
    serve_down, scale_down = served(w_down, avg_down, 2, 1)
    part_router = (router_weight * router_gain[:, None]).astype(jnp.bfloat16)
    row_router = lax.all_gather(part_router, "rows", axis=0, tiled=True)
    serve_router = lax.all_gather(row_router, "owner", axis=1, tiled=True)
    return (serve_gate, serve_up, serve_down, scale_gate, scale_up, scale_down, serve_router)


def solution(mesh):
    parts = mesh.shape["rows"]

    def dispatched(*args):
        experts, high, wide = args[0].shape
        tall, deep = args[4].shape[1:]
        block, slab = wide // parts, tall // parts
        aligned = block == LANES and slab % LANES == 0 and deep % LANES == 0
        aligned = aligned and slab * deep == high * block and experts % STEP == 0
        aligned = aligned and experts >= 2 * STEP and args[6].size % wide == 0
        return shards(parts, *args) if aligned else plain_shards(*args)

    return jax.shard_map(
        dispatched,
        mesh=mesh,
        in_specs=(
            P("owner", "rows", None),
            P("owner", "rows", None),
            P("owner", "rows", None),
            P("owner", "rows", None),
            P("owner", None, "rows"),
            P("owner", None, "rows"),
            P("rows", "owner"),
            P("rows"),
        ),
        out_specs=(
            P("owner", None, "rows"),
            P("owner", None, "rows"),
            P("owner", "rows", None),
            P("owner", "rows"),
            P("owner", "rows"),
            P("owner", "rows"),
            P(),
        ),
        check_vma=False,
    )
```

time: 827 us -> 625 us (0.76)
  blocking collectives: 199 us -> 25.5 us
  local copies, waits for them, and re-layouts: 114 us -> 3.84 us
  Pallas kernels: 0 us -> 97.2 us
  other arithmetic: 86.1 us -> 2.34 us
  waiting for transfers between devices: 397 us -> 466 us
    all_gather x2, blocking collectives: 199 us -> 25.5 us  [the longest x1 16.5 us: shards(): lax.all_gather(jnp.concatenate((head, part_router.reshape(-1, 1, wide))),...]
    pallas_call x0 -> x14, Pallas kernels: none -> 97.2 us  [call(): pl.pallas_call(body, grid=(count // STEP,), in_specs=list(specs), out_spe...]
    all_to_all x3, waiting for transfers between devices: 331 us -> 405 us  [exchanged(): return lax.all_to_all(x, 'rows', split_axis=0, concat_axis=0, tiled=True)]
    unnamed x20 -> x2, local copies, waits for them, and re-layouts: 62.9 us -> 0.72 us
    all_to_all x4 -> x0, local copies, waits for them, and re-layouts: 49.4 us -> none  [the longest x2 24.8 us: shards(): lax.all_to_all(narrow_down, 'rows', split_axis=1, concat_axis=2, tiled=True)]
    convert_element_type x4 -> x0, other arithmetic: 47.7 us -> none  [the longest x1 23.8 us: shards(): (fresh_down / jnp.expand_dims(scale_down, 2)).astype(jnp.bfloat16)]
    reduce_sum x2 -> x1, other arithmetic: 38.4 us -> 0.24 us  [shards(): scale_head = jnp.sqrt(jnp.sum(gathered[:, :early], axis=0))]
  transfers between devices with their start and end apart: 4 -> 4, of which waited for: 3 -> 4; matrix products, arithmetic and copies ran while one was open for 8% -> 1% of each run, Pallas kernels for 0% -> 12%
where the time goes in v1:
time: 625 us; the launch traced here: 624 us
  waiting for transfers between devices  466 us (75%)
  Pallas kernels  97.2 us (16%)
  blocking collectives  25.5 us (4%)
  starting transfers between devices  15 us (2%)
  between operations  14.2 us (2%)
    all_to_all x3, waiting for transfers between devices, exchanged(): return lax.all_to_all(x, 'rows', split_axis=0, concat_axis=0, tiled=True)  405 us
    pallas_call x14, Pallas kernels, call(): pl.pallas_call(body, grid=(count // STEP,), in_specs=list(specs), out_spe...  97.2 us
    psum x1, waiting for transfers between devices, shards(): lax.psum((jnp.concatenate((part_up, part_rest)), part_down), 'rows')  61.4 us
    all_gather x1, blocking collectives, shards(): lax.all_gather(jnp.concatenate((head, part_router.reshape(-1, 1, wide))),...  16.5 us
    all_to_all x3, starting transfers between devices, exchanged(): return lax.all_to_all(x, 'rows', split_axis=0, concat_axis=0, tiled=True)  14.9 us
  transfers between devices with their start and end apart: 4, of which 4 were waited for; matrix products, arithmetic and copies ran while one was open for 1% of the time, Pallas kernels for 12%

profile of v1, /device:TPU:0, one launch (start us, length us, event | category | flops | bytes accessed | tf_op | source)
XLA Modules:
  0.0 624.2 jit_solution(1997259938808066041)
XLA Ops:
  7.2 0.7 convert_bitcast_fusion
  7.9 7.9 %shard_map.135 = f32[12,1,1024]{2,1,0:T(1,128)S(1)} custom-call(f32[16,256,1024]{2,1,0:T(8,128)} %w.7, bf16[16,256,1024]{2,1,0:T(8,128)(2,1)} %a.7), custom_call_target="tpu_custom_call" | custom-call | flops 25165824 | bytes 25165824 | tf_op jit(solution)/shard_map/pallas_call | solution.py:93
  15.8 0.1 pad_maximum_fusion.1
  15.9 16.5 %all-gather = f32[128,1,1024]{2,1,0:T(1,128)S(1)} all-gather(f32[16,1,1024]{2,1,0:T(1,128)S(1)} %pad_maximum_fusion.1), channel_id=2, replica_groups=mesh['owner'=4,'rows'=8] {'rows'}, dimensions={0}, use_global_device_ids=true | all-gather | bytes 589824 | tf_op jit(solution)/shard_map/all_gather | solution.py:140
  32.4 0.2 slice_reduce_fusion
  32.7 10.0 %shard_map.136 = bf16[8,12,256,128]{3,2,1,0:T(8,128)(2,1)} custom-call(f32[16,256,1024]{2,1,0:T(8,128)} %w.7, bf16[16,256,1024]{2,1,0:T(8,128)(2,1)} %a.7, f32[12,1,1024]{2,1,0:T(1,128)S(1)} %sqrt.12.s), custom_call_target="tpu_custom_call" | custom-call | flops 25165824 | bytes 25165824 | tf_op jit(solution)/shard_map/pallas_call | solution.py:93
  42.7 4.8 all-to-all-start.1
  47.5 0.0 all-reduce.3.cloned.1.call-start
  47.6 3.9 shard_map.139
  51.4 9.8 %shard_map.138 = f32[16,1,1024]{2,1,0:T(1,128)S(1)} custom-call(f32[16,256,1024]{2,1,0:T(8,128)} %w.8, bf16[16,256,1024]{2,1,0:T(8,128)(2,1)} %a.8), custom_call_target="tpu_custom_call" | custom-call | flops 33554432 | bytes 33554432 | tf_op jit(solution)/shard_map/pallas_call | solution.py:93
  61.2 10.1 %shard_map.137 = f32[16,1,1024]{2,1,0:T(1,128)} custom-call(f32[16,1024,256]{2,1,0:T(8,128)} %w.10, bf16[16,1024,256]{2,1,0:T(8,128)(2,1)} %a.10), custom_call_target="tpu_custom_call" | custom-call | flops 33554432 | bytes 33554432 | tf_op jit(solution)/shard_map/pallas_call | solution.py:93
  71.3 0.7 pad_maximum_fusion
  72.0 0.0 all-reduce.3.cloned.1.call-update
  72.0 61.4 %all-reduce.3.cloned.1.call-done = (f32[16,1,1024]{2,1,0:T(1,128)}, f32[20,1,1024]{2,1,0:T(1,128)}) async-done(((f32[16,1,1024]{2,1,0:T(1,128)}, f32[20,1,1024]{2,1,0:T(1,128)}), (f32[16,1,1024]{2,1,0:T(1,128)}, f32[20,1,1024]{2,1,0:T(1,128)})) %all-reduce.3.cloned.1.call-update) | async-done | bytes 147472 | tf_op jit(solution)/shard_map/psum | solution.py:157
  133.5 1.0 sqrt.14.s
  134.5 1.0 sqrt.13.s
  135.5 4.8 shard_map.140.refs_0_
  140.3 12.1 %shard_map.141.refs_0_ = bf16[8,28,256,128]{3,2,1,0:T(8,128)(2,1)} custom-call(f32[16,256,1024]{2,1,0:T(8,128)} %w.8, bf16[16,256,1024]{2,1,0:T(8,128)(2,1)} %a.8, f32[20,1,1024]{2,1,0:T(1,128)S(1)} %sqrt.14.s, bf16[8,28,256,128]{3,2,1,0:T(8,128)(2,1)} %shard_map.140.refs_0_), custom_call_target="tpu_custom_call", output_to_operand_aliasing={{}: (3, {})} | custom-call | flops 33554432 | bytes 33554432 | tf_op jit(solution)/shard_map/pallas_call | solution.py:93
  152.4 6.9 %shard_map.142 = bf16[8,28,256,128]{3,2,1,0:T(8,128)(2,1)} custom-call(f32[16,1024,256]{2,1,0:T(8,128)} %w.10, bf16[16,1024,256]{2,1,0:T(8,128)(2,1)} %a.10, f32[16,1,1024]{2,1,0:T(1,128)S(1)} %sqrt.13.s, bf16[8,28,256,128]{3,2,1,0:T(8,128)(2,1)} %shard_map.141.refs_0_), custom_call_target="tpu_custom_call", output_to_operand_aliasing={{}: (3, {})} | custom-call | flops 16777216 | bytes 16777216 | tf_op jit(solution)/shard_map/pallas_call | solution.py:93
  159.2 30.5 %all-to-all-done.1.x = bf16[8,12,256,128]{3,2,1,0:T(8,128)(2,1)} async-done(((bf16[8,12,256,128]{3,2,1,0:T(8,128)(2,1)}), bf16[8,12,256,128]{3,2,1,0:T(8,128)(2,1)}, u32[]{:S(2)}, u32[]{:S(2)}) %all-to-all-start.1) | async-done | bytes 6291488 | tf_op jit(solution)/shard_map/all_to_all | solution.py:125
  189.7 5.6 all-to-all-start
  195.3 0.4 slice_reduce_fusion.1
  195.7 6.9 %shard_map.146 = bf16[8,8,256,128]{3,2,1,0:T(8,128)(2,1)} custom-call(f32[16,1024,256]{2,1,0:T(8,128)} %w.10, bf16[16,1024,256]{2,1,0:T(8,128)(2,1)} %a.10, f32[16,1,1024]{2,1,0:T(1,128)S(1)} %sqrt.13.s), custom_call_target="tpu_custom_call" | custom-call | flops 16777216 | bytes 16777216 | tf_op jit(solution)/shard_map/pallas_call | solution.py:93
  202.6 311.4 %all-to-all-done.x = bf16[8,28,256,128]{3,2,1,0:T(8,128)(2,1)} async-done(((bf16[8,28,256,128]{3,2,1,0:T(8,128)(2,1)}), bf16[8,28,256,128]{3,2,1,0:T(8,128)(2,1)}, u32[]{:S(2)}, u32[]{:S(2)}) %all-to-all-start) | async-done | bytes 14680096 | tf_op jit(solution)/shard_map/all_to_all | solution.py:125
  514.0 4.6 all-to-all-start.2
  518.7 9.0 %all_gather.11 = bf16[64,2048]{1,0:T(8,128)(2,1)S(1)} all-gather(bf16[16,2048]{1,0:T(8,128)(2,1)S(1)} %bitcast.13), channel_id=1, replica_groups=mesh['owner'=4,'rows'=8] {'owner'}, dimensions={0}, use_global_device_ids=true | all-gather | bytes 327680 | tf_op jit(solution)/shard_map/all_gather | solution.py:181
  527.6 0.6 constant_dynamic-slice_fusion.1
  528.3 0.6 fusion
  528.9 6.4 %shard_map.143.refs_0_ = bf16[16,2048,128]{2,1,0:T(8,128)(2,1)} custom-call(bf16[8,12,256,128]{3,2,1,0:T(8,128)(2,1)} %all-to-all-done.1.x), custom_call_target="tpu_custom_call" | custom-call | flops 25165824 | bytes 25165824 | tf_op jit(solution)/shard_map/pallas_call | solution.py:93
  535.3 3.0 shard_map.144
  538.3 4.1 shard_map.147.refs_0_
  542.5 7.1 %shard_map.145 = bf16[16,2048,128]{2,1,0:T(8,128)(2,1)} custom-call(bf16[8,28,256,128]{3,2,1,0:T(8,128)(2,1)} %all-to-all-done.x), custom_call_target="tpu_custom_call" | custom-call | flops 33554432 | bytes 33554432 | tf_op jit(solution)/shard_map/pallas_call | solution.py:93
  549.6 62.9 %all-to-all-done.2.x = bf16[8,8,256,128]{3,2,1,0:T(8,128)(2,1)} async-done(((bf16[8,8,256,128]{3,2,1,0:T(8,128)(2,1)}), bf16[8,8,256,128]{3,2,1,0:T(8,128)(2,1)}, u32[]{:S(2)}, u32[]{:S(2)}) %all-to-all-start.2) | async-done | bytes 4194336 | tf_op jit(solution)/shard_map/all_to_all | solution.py:125
  612.6 4.1 shard_map.148
  616.7 0.7 copy.31
  (8 shorter events, 0.2 us)
Async XLA Ops:
  42.7 147.0 %all-to-all-start.1 = ((bf16[8,12,256,128]{3,2,1,0:T(8,128)(2,1)}), bf16[8,12,256,128]{3,2,1,0:T(8,128)(2,1)}, u32[]{:S(2)}, u32[]{:S(2)}) async-start(bf16[8,12,256,128]{3,2,1,0:T(8,128)(2,1)} %shard_map.136), calls=%async_computation.1 | async-start | bytes 12582912 | tf_op jit(solution)/shard_map/all_to_all | solution.py:125
  47.5 86.0 %all-reduce.3.cloned.1.call-start = ((), (), s32[]{:S(2)}) async-start(), calls=%async_computation.3 | async-start | bytes 294912 | tf_op jit(solution)/shard_map/psum | solution.py:157
  189.7 324.2 %all-to-all-start = ((bf16[8,28,256,128]{3,2,1,0:T(8,128)(2,1)}), bf16[8,28,256,128]{3,2,1,0:T(8,128)(2,1)}, u32[]{:S(2)}, u32[]{:S(2)}) async-start(bf16[8,28,256,128]{3,2,1,0:T(8,128)(2,1)} %shard_map.142), calls=%async_computation | async-start | bytes 29360128 | tf_op jit(solution)/shard_map/all_to_all | solution.py:125
  514.0 98.6 %all-to-all-start.2 = ((bf16[8,8,256,128]{3,2,1,0:T(8,128)(2,1)}), bf16[8,8,256,128]{3,2,1,0:T(8,128)(2,1)}, u32[]{:S(2)}, u32[]{:S(2)}) async-start(bf16[8,8,256,128]{3,2,1,0:T(8,128)(2,1)} %shard_map.146), calls=%async_computation.2 | async-start | bytes 8388608 | tf_op jit(solution)/shard_map/all_to_all | solution.py:125
Sparse Core Ops, SparseCore 0:
  72.2 61.2 all-reduce.2
